TPU v7x, 256 devices: a 8x8x2 block of a 8x8x16 slice. The times are simulated.
256 devices in a mesh: groups: 2 (over z), section: 2 (over core), mesh: 64 (over x, y).
Axes of the slice: x: 8, y: 8, z: 2, core: 2. Of those that a mesh axis runs over, the one named last changes fastest.
The devices are a block of a 8x8x16 slice.
Arguments:
- inputs: bfloat16 [4, 128, 8192], P('groups', None, 'mesh'), parts along dimension 0, may hold values from -12 to 12
- segments: int32 [4, 128], P('groups'), parts along dimension 0, may hold values from 0 to 3, never falling along the last dimension, each value on 1 to 64 neighbouring positions
- gains: bfloat16 [2, 1, 8192], P('section'), may hold values from 0.25 to 1.75
- w_query: bfloat16 [2, 1, 8192, 8192], P('section', None, None, 'mesh'), may hold values from -1.3258252 to 1.3258252
- w_keyval: bfloat16 [2, 1, 8192, 2048], P('section', None, None, 'mesh'), may hold values from -0.055242717 to 0.055242717
- w_output: bfloat16 [2, 1, 8192, 8192], P('section', None, None, 'mesh'), may hold values from -0.0625 to 0.0625
Outputs:
- section_outputs: bfloat16 [2, 4, 128, 8192], P('section', 'groups', None, 'mesh'), parts along dimension 1
There are 2 independent parts, one for each index of `groups`. A program takes and returns all parts, laid end to end along the dimension named above; an argument that names none is the same for every part. Nothing has to cross between parts.
Inputs may be any that keep to these rules, and one draw needn't show every extreme that they name: `segments`: along each micro-batch the document ids never fall; each document spans 1 to 64 positions.
All inputs are finite; a program needn't handle non-finite values.
Results may differ from a plain program's by a relative error of at most 0.0052.
Values may be sent and summed in bfloat16 or wider, within the bound.
No kernel may reach another device: no remote copies, remote signals or barrier semaphores. Data moves between devices by JAX's collectives and lax.ppermute only.
A program may use at most 64 MiB of HBM per device.

v0:
```python
import jax
import jax.numpy as jnp
from jax import lax
from jax.sharding import Mesh
from jax.sharding import PartitionSpec as P

HD = 128
GROUP = 8
MESH = ("mesh_0", "mesh_1")
norm_epsilon = 1e-05
rope_theta = 500000.0


def joined_along(parts, dim):
    lengths = list(parts.shape[1:])
    lengths[dim] *= parts.shape[0]
    return jnp.moveaxis(parts, 0, dim).reshape(lengths)


def gather_in_order(x, axes, sequence):
    parts = x[None]
    for k in sequence:
        parts = lax.all_gather(parts, axes[k], axis=0, tiled=True)
    block = [lax.axis_size(axes[k]) for k in reversed(sequence)]
    parts = parts.reshape(*block, *x.shape)
    turned = sorted(range(len(sequence)), key=lambda place: sequence[len(sequence) - 1 - place])
    return parts.transpose(*turned, *range(len(sequence), parts.ndim)).reshape(-1, *x.shape)


def whole_of(x, axes, sequence, dim):
    return joined_along(gather_in_order(x, axes, sequence), dim)


def partner_2(x, axis, distance):
    return lax.ppermute(x, axis, [(i, i ^ 1 << distance) for i in range(lax.axis_size(axis))])


def from_behind(block, axis, distance):
    devices = range(lax.axis_size(axis))
    route = [(i - distance, i) for i in devices if i - distance in devices]
    return lax.ppermute(block, axis, route)


def position_tables(segment_row):
    row_length = segment_row.shape[0]
    indices = jnp.arange(row_length, dtype=jnp.int32)
    doc_starts = jnp.concatenate([jnp.ones((1,), dtype=bool), segment_row[1:] != segment_row[:-1]])
    first_index = lax.cummax(jnp.where(doc_starts, indices, jnp.zeros_like(indices)), axis=0)
    positions = (indices - first_index).astype(jnp.float32)
    half_width = HD // 2
    freqs = rope_theta ** (-(2.0 * jnp.arange(half_width, dtype=jnp.float32)) / HD)
    angles = positions[:, None] * freqs[None, :]
    cosine_table = jnp.concatenate([jnp.cos(angles), jnp.cos(angles)], axis=1)
    sine_table = jnp.concatenate([jnp.sin(angles), jnp.sin(angles)], axis=1)
    allowed = (indices[None, :] <= indices[:, None]) & (
        segment_row[None, :] == segment_row[:, None]
    )
    return (cosine_table, sine_table, allowed)


def rotate(values, cosine_table, sine_table):
    half_width = values.shape[-1] // 2
    turned = jnp.concatenate([-values[..., half_width:], values[..., :half_width]], axis=-1)
    return values * cosine_table + turned * sine_table


def softmax_weights(scores, allowed):
    masked = jnp.where(allowed, scores, -1e30)
    highest = jnp.max(masked, axis=-1, keepdims=True)
    raised = jnp.exp(masked - highest)
    return (raised / jnp.sum(raised, axis=-1, keepdims=True)).astype(jnp.bfloat16)


def apply_layer(
    activations,
    gain_row,
    query_weight,
    keyval_weight,
    output_weight,
    cosine_table,
    sine_table,
    allowed,
    mesh_index,
):
    floats = activations.astype(jnp.float32)
    gathered = whole_of(activations, MESH, (0, 1), 1)
    whole_floats = gathered.astype(jnp.float32)
    scale = lax.rsqrt(jnp.mean(whole_floats * whole_floats, axis=1, keepdims=True) + norm_epsilon)
    normed = (whole_floats * scale * gain_row.astype(jnp.float32)).astype(jnp.bfloat16)
    query_raw = jnp.dot(normed, query_weight, preferred_element_type=jnp.float32)
    keyval_raw = jnp.dot(normed, keyval_weight, preferred_element_type=jnp.float32)
    query = rotate(query_raw, cosine_table, sine_table).astype(jnp.bfloat16)
    keyval_part = keyval_raw.astype(jnp.bfloat16)
    for bit_index in range(GROUP.bit_length() - 1):
        partner = partner_2(keyval_part, MESH, bit_index)
        upper_half = mesh_index // (1 << bit_index) % 2 == 1
        keyval_part = jnp.where(
            upper_half,
            jnp.concatenate([partner, keyval_part], axis=1),
            jnp.concatenate([keyval_part, partner], axis=1),
        )
    keys = rotate(keyval_part[:, :HD].astype(jnp.float32), cosine_table, sine_table).astype(
        jnp.bfloat16
    )
    values = keyval_part[:, HD:]
    scores = jnp.dot(query, keys.T, preferred_element_type=jnp.float32) * HD ** (-0.5)
    probs = softmax_weights(scores, allowed)
    attended = jnp.dot(probs, values, preferred_element_type=jnp.float32).astype(jnp.bfloat16)
    mixed = jnp.dot(
        whole_of(attended, MESH, (0, 1), 1), output_weight, preferred_element_type=jnp.float32
    )
    return (floats + mixed).astype(jnp.bfloat16)


def shards(inputs, segments, gains, w_query, w_keyval, w_output):
    micro_count, row_count, local_cols = inputs.shape
    section_count = lax.axis_size("section")
    section_index = lax.axis_index("section")
    mesh_index = lax.axis_index(MESH)
    cosine_list, sine_list, allowed_list = ([], [], [])
    for micro_index in range(micro_count):
        cosine_table, sine_table, allowed = position_tables(segments[micro_index])
        cosine_list.append(cosine_table)
        sine_list.append(sine_table)
        allowed_list.append(allowed)
    cosine_all = jnp.stack(cosine_list)
    sine_all = jnp.stack(sine_list)
    allowed_all = jnp.stack(allowed_list)
    step_count = micro_count + section_count - 1
    received = jnp.zeros((row_count, local_cols), jnp.bfloat16)
    results = []
    for section_step in range(step_count):
        feed_slot = min(section_step, micro_count - 1)
        micro_here = jnp.clip(section_step - section_index, 0, micro_count - 1)
        cosine_table = lax.dynamic_index_in_dim(cosine_all, micro_here, 0, keepdims=False)
        sine_table = lax.dynamic_index_in_dim(sine_all, micro_here, 0, keepdims=False)
        allowed = lax.dynamic_index_in_dim(allowed_all, micro_here, 0, keepdims=False)
        current = jnp.where(section_index == 0, inputs[feed_slot], received)
        current = apply_layer(
            current,
            gains[0, 0],
            w_query[0, 0],
            w_keyval[0, 0],
            w_output[0, 0],
            cosine_table,
            sine_table,
            allowed,
            mesh_index,
        )
        results.append(current)
        if section_step + 1 < step_count:
            received = from_behind(current, "section", 1)
    stacked = jnp.stack(results)
    chosen = lax.dynamic_slice_in_dim(stacked, section_index, micro_count, 0)
    return chosen[None]


def solution(mesh):
    finer = Mesh(
        mesh.devices.reshape(mesh.shape["groups"], mesh.shape["section"], 8, 8),
        ("groups", "section", "mesh_0", "mesh_1"),
    )
    in_specs = (
        P("groups", None, MESH),
        P("groups", None),
        P("section", None, None),
        P("section", None, None, MESH),
        P("section", None, None, MESH),
        P("section", None, None, MESH),
    )
    out_specs = P("section", "groups", None, MESH)
    return jax.shard_map(
        shards, mesh=finer, in_specs=in_specs, out_specs=out_specs, check_vma=False
    )
```

profile of v0, /device:TPU:514, one launch (start us, length us, event | category | flops | bytes accessed | tf_op | source)
XLA Modules:
  0.0 562.5 jit_solution(12271159927433915738)
XLA Ops:
  7.5 43.0 %all_gather.36 = bf16[8,128,128]{2,1,0:T(8,128)(2,1)} all-gather(bf16[1,128,128]{2,1,0:T(8,128)(2,1)S(1)} %slice_select_fusion), channel_id=1, replica_groups=mesh['groups'=2,'section'=2,'mesh_0'=8,'mesh_1'=8] {'mesh_0'}, dimensions={0}, use_global_device_ids=true | all-gather | bytes 294912 | tf_op jit(solution)/shard_map/all_gather | solution.py:23
  54.5 40.1 %all-gather.12.cloned.1.call-done = bf16[64,128,128]{2,1,0:T(8,128)(2,1)} async-done(((bf16[8,128,128]{2,1,0:T(8,128)(2,1)}), bf16[64,128,128]{2,1,0:T(8,128)(2,1)}) %all-gather.12.cloned.1.call-update) | async-done | bytes 2097168 | tf_op jit(solution)/shard_map/all_gather | solution.py:23
  99.7 4.1 copy.46
  111.3 2.4 fusion.19
  114.4 3.2 collective-permute-start.2
  117.7 4.7 collective-permute-done.2
  122.9 27.0 %all-gather = bf16[1024,128]{1,0:T(8,128)(2,1)} all-gather(bf16[128,128]{1,0:T(8,128)(2,1)S(1)} %convolution_convert_fusion.2), channel_id=2, replica_groups=mesh['groups'=2,'section'=2,'mesh_0'=8,'mesh_1'=8] {'mesh_0'}, dimensions={0}, use_global_device_ids=true | all-gather | bytes 294912 | tf_op jit(solution)/shard_map/all_gather | solution.py:23
  150.0 41.0 %all-gather.14.cloned.1.call-done = bf16[64,128,128]{2,1,0:T(8,128)(2,1)} async-done(((bf16[8,128,128]{2,1,0:T(8,128)(2,1)}), bf16[64,128,128]{2,1,0:T(8,128)(2,1)}) %all-gather.14.cloned.1.call-update) | async-done | bytes 2097168 | tf_op jit(solution)/shard_map/all_gather | solution.py:23
  191.0 3.1 copy.49
  194.1 4.1 copy.50
  198.2 3.0 fusion.27
  203.4 27.0 %all-gather.1 = bf16[1024,128]{1,0:T(8,128)(2,1)} all-gather(bf16[128,128]{1,0:T(8,128)(2,1)S(1)} %bitcast_select_fusion.1), channel_id=3, replica_groups=mesh['groups'=2,'section'=2,'mesh_0'=8,'mesh_1'=8] {'mesh_0'}, dimensions={0}, use_global_device_ids=true | all-gather | bytes 294912 | tf_op jit(solution)/shard_map/all_gather | solution.py:23
  230.7 40.7 %all-gather.16.cloned.1.call-done = bf16[64,128,128]{2,1,0:T(8,128)(2,1)} async-done(((bf16[8,128,128]{2,1,0:T(8,128)(2,1)}), bf16[64,128,128]{2,1,0:T(8,128)(2,1)}) %all-gather.16.cloned.1.call-update) | async-done | bytes 2097168 | tf_op jit(solution)/shard_map/all_gather | solution.py:23
  276.6 4.1 copy.52
  288.1 2.4 fusion.17
  291.3 3.2 collective-permute-start.6
  294.5 4.7 collective-permute-done.6
  299.7 27.0 %all-gather.2 = bf16[1024,128]{1,0:T(8,128)(2,1)} all-gather(bf16[128,128]{1,0:T(8,128)(2,1)S(1)} %convolution_convert_fusion.1), channel_id=4, replica_groups=mesh['groups'=2,'section'=2,'mesh_0'=8,'mesh_1'=8] {'mesh_0'}, dimensions={0}, use_global_device_ids=true | all-gather | bytes 294912 | tf_op jit(solution)/shard_map/all_gather | solution.py:23
  326.8 41.0 %all-gather.18.cloned.1.call-done = bf16[64,128,128]{2,1,0:T(8,128)(2,1)} async-done(((bf16[8,128,128]{2,1,0:T(8,128)(2,1)}), bf16[64,128,128]{2,1,0:T(8,128)(2,1)}) %all-gather.18.cloned.1.call-update) | async-done | bytes 2097168 | tf_op jit(solution)/shard_map/all_gather | solution.py:23
  367.8 3.1 copy.53
  371.0 4.1 copy.54
  375.0 3.0 add_convert_fusion.1
  380.2 27.0 %all-gather.3 = bf16[1024,128]{1,0:T(8,128)(2,1)} all-gather(bf16[128,128]{1,0:T(8,128)(2,1)S(1)} %bitcast_select_fusion), channel_id=5, replica_groups=mesh['groups'=2,'section'=2,'mesh_0'=8,'mesh_1'=8] {'mesh_0'}, dimensions={0}, use_global_device_ids=true | all-gather | bytes 294912 | tf_op jit(solution)/shard_map/all_gather | solution.py:23
  407.3 40.9 %all-gather.20.cloned.1.call-done = bf16[64,128,128]{2,1,0:T(8,128)(2,1)} async-done(((bf16[8,128,128]{2,1,0:T(8,128)(2,1)}), bf16[64,128,128]{2,1,0:T(8,128)(2,1)}) %all-gather.20.cloned.1.call-update) | async-done | bytes 2097168 | tf_op jit(solution)/shard_map/all_gather | solution.py:23
  453.3 4.1 copy.56
  468.2 3.2 collective-permute-start.10
  471.4 4.7 collective-permute-done.10
  476.7 27.0 %all-gather.4 = bf16[1024,128]{1,0:T(8,128)(2,1)} all-gather(bf16[128,128]{1,0:T(8,128)(2,1)S(1)} %convolution_convert_fusion), channel_id=6, replica_groups=mesh['groups'=2,'section'=2,'mesh_0'=8,'mesh_1'=8] {'mesh_0'}, dimensions={0}, use_global_device_ids=true | all-gather | bytes 294912 | tf_op jit(solution)/shard_map/all_gather | solution.py:23
  503.7 41.0 %all-gather.22.cloned.1.call-done = bf16[64,128,128]{2,1,0:T(8,128)(2,1)} async-done(((bf16[8,128,128]{2,1,0:T(8,128)(2,1)}), bf16[64,128,128]{2,1,0:T(8,128)(2,1)}) %all-gather.22.cloned.1.call-update) | async-done | bytes 2097168 | tf_op jit(solution)/shard_map/all_gather | solution.py:23
  544.7 3.1 copy.57
  547.9 4.1 copy.58
  551.9 3.0 fusion.71
  (103 shorter events, 54.8 us)
Async XLA Ops:
  6.5 104.7 %copy-start = (bf16[1,1,8192,128]{3,2,1,0:T(8,128)(2,1)S(1)}, bf16[1,1,8192,128]{3,2,1,0:T(8,128)(2,1)}, u32[]{:S(2)}) copy-start(bf16[1,1,8192,128]{3,2,1,0:T(8,128)(2,1)} %param.9) | copy-start | bytes 6291460
  6.6 88.0 %all-gather.12.cloned.1.call-start = ((), (), s32[]{:S(2)}) async-start(), calls=%async_computation | async-start | bytes 2359296 | tf_op jit(solution)/shard_map/all_gather | solution.py:23
  50.6 140.4 %all-gather.14.cloned.1.call-start = ((), (), s32[]{:S(2)}) async-start(), calls=%async_computation.1 | async-start | bytes 2359296 | tf_op jit(solution)/shard_map/all_gather | solution.py:23
  99.7 4.1 copy-start.1
  105.9 3.8 collective-permute-start
  109.7 4.8 collective-permute-start.1
  114.4 7.9 %collective-permute-start.2 = (bf16[128,128]{0,1:T(8,128)(2,1)S(1)}, bf16[128,128]{0,1:T(8,128)(2,1)S(1)}, u32[]{:S(2)}, u32[]{:S(2)}) collective-permute-start(bf16[128,128]{0,1:T(8,128)(2,1)S(1)} %maximum_select_fusion.3), channel_id=1, source_target_pairs={{0,4},{1,5},{2,6},{3,7},{4,0},{5,1},{6,2},{7,3},{8,12},{9,13},{10,... | collective-permute-start | bytes 98312 | tf_op jit(solution)/shard_map/ppermute | solution.py:35
  150.0 121.4 %all-gather.16.cloned.1.call-start = ((), (), s32[]{:S(2)}) async-start(), calls=%async_computation.2 | async-start | bytes 2359296 | tf_op jit(solution)/shard_map/all_gather | solution.py:23
  198.2 5.2 copy-start.2
  201.2 2.2 collective-permute-start.3
  230.5 137.3 %all-gather.18.cloned.1.call-start = ((), (), s32[]{:S(2)}) async-start(), calls=%async_computation.3 | async-start | bytes 2359296 | tf_op jit(solution)/shard_map/all_gather | solution.py:23
  282.7 3.8 collective-permute-start.4
  286.5 4.8 collective-permute-start.5
  291.3 7.9 %collective-permute-start.6 = (bf16[128,128]{0,1:T(8,128)(2,1)S(1)}, bf16[128,128]{0,1:T(8,128)(2,1)S(1)}, u32[]{:S(2)}, u32[]{:S(2)}) collective-permute-start(bf16[128,128]{0,1:T(8,128)(2,1)S(1)} %maximum_select_fusion.4), channel_id=1, source_target_pairs={{0,4},{1,5},{2,6},{3,7},{4,0},{5,1},{6,2},{7,3},{8,12},{9,13},{10,... | collective-permute-start | bytes 98312 | tf_op jit(solution)/shard_map/ppermute | solution.py:35
  326.8 121.3 %all-gather.20.cloned.1.call-start = ((), (), s32[]{:S(2)}) async-start(), calls=%async_computation.4 | async-start | bytes 2359296 | tf_op jit(solution)/shard_map/all_gather | solution.py:23
  378.0 2.2 collective-permute-start.7
  407.2 137.5 %all-gather.22.cloned.1.call-start = ((), (), s32[]{:S(2)}) async-start(), calls=%async_computation.5 | async-start | bytes 2359296 | tf_op jit(solution)/shard_map/all_gather | solution.py:23
  459.4 3.8 collective-permute-start.8
  463.2 5.0 collective-permute-start.9
  468.2 7.9 %collective-permute-start.10 = (bf16[128,128]{0,1:T(8,128)(2,1)S(1)}, bf16[128,128]{0,1:T(8,128)(2,1)S(1)}, u32[]{:S(2)}, u32[]{:S(2)}) collective-permute-start(bf16[128,128]{0,1:T(8,128)(2,1)S(1)} %maximum_select_fusion.5), channel_id=1, source_target_pairs={{0,4},{1,5},{2,6},{3,7},{4,0},{5,1},{6,2},{7,3},{8,12},{9,13},{10,... | collective-permute-start | bytes 98312 | tf_op jit(solution)/shard_map/ppermute | solution.py:35
Sparse Core Ops, SparseCore 0:
  50.7 43.8 all-gather.11
  150.1 40.8 all-gather.13
  230.6 40.7 all-gather.15
  326.9 40.8 all-gather.17
  407.3 40.7 all-gather.19
  503.8 40.8 all-gather.21
where the time goes:
time: 564 us; the launch traced here: 562 us
  waiting for transfers between devices  270 us (48%)
  blocking collectives  178 us (32%)
  local copies, waits for them, and re-layouts  36.4 us (6%)
  matrix products  23.5 us (4%)
  starting transfers between devices  22.3 us (4%)
  other arithmetic  18.8 us (3%)
  between operations  13.8 us (2%)
    all_gather x6, waiting for transfers between devices, gather_in_order(): parts = lax.all_gather(parts, axes[k], axis=0, tiled=True)  245 us
    all_gather x6, blocking collectives, gather_in_order(): parts = lax.all_gather(parts, axes[k], axis=0, tiled=True)  178 us
    ppermute x9, waiting for transfers between devices, partner_2(): lax.ppermute(x, axis, [(i, i ^ 1 << distance) for i in range(lax.axis_siz...  23.4 us
    ppermute x9, starting transfers between devices, partner_2(): lax.ppermute(x, axis, [(i, i ^ 1 << distance) for i in range(lax.axis_siz...  19.2 us
    convert_element_type x3, local copies, waits for them, and re-layouts, apply_layer(): (whole_floats * scale * gain_row.astype(jnp.float32)).astype(jnp.bfloat16)  12.2 us
    transpose x3, local copies, waits for them, and re-layouts, joined_along(): return jnp.moveaxis(parts, 0, dim).reshape(lengths)  12.2 us
  transfers between devices with their start and end apart: 17, of which 17 were waited for; matrix products, arithmetic and copies ran while one was open for 2% of the time, Pallas kernels for 0%

commit v1 on v0

--- a/solution.py
+++ b/solution.py
@@ -20,7 +20,9 @@
 def gather_in_order(x, axes, sequence):
     parts = x[None]
     for k in sequence:
-        parts = lax.all_gather(parts, axes[k], axis=0, tiled=True)
+        parts = jnp.concatenate(
+            lax.all_to_all(jnp.stack([parts] * lax.axis_size(axes[k])), axes[k], 0, 0), axis=0
+        )
     block = [lax.axis_size(axes[k]) for k in reversed(sequence)]
     parts = parts.reshape(*block, *x.shape)
     turned = sorted(range(len(sequence)), key=lambda place: sequence[len(sequence) - 1 - place])

time: 564 us -> 533 us (0.945)
  waiting for transfers between devices: 270 us -> 129 us
  blocking collectives: 178 us -> 305 us
  between operations: 13.8 us -> 0.4 us
    all_to_all x0 -> x10, blocking collectives: none -> 305 us  [gather_in_order(): lax.all_to_all(jnp.stack([parts] * lax.axis_size(axes[k])), axes[k], 0, 0)]
    all_gather x6 -> x0, waiting for transfers between devices: 245 us -> none  [gather_in_order(): parts = lax.all_gather(parts, axes[k], axis=0, tiled=True)]
    all_gather x6 -> x0, blocking collectives: 178 us -> none  [gather_in_order(): parts = lax.all_gather(parts, axes[k], axis=0, tiled=True)]
    all_to_all x0 -> x2, waiting for transfers between devices: none -> 89.8 us  [gather_in_order(): lax.all_to_all(jnp.stack([parts] * lax.axis_size(axes[k])), axes[k], 0, 0)]
    ppermute x9, waiting for transfers between devices: 23.4 us -> 37.9 us  [partner_2(): lax.ppermute(x, axis, [(i, i ^ 1 << distance) for i in range(lax.axis_siz...]
    ppermute x9, starting transfers between devices: 19.2 us -> 5.1 us  [partner_2(): lax.ppermute(x, axis, [(i, i ^ 1 << distance) for i in range(lax.axis_siz...]
    transpose x3 -> x0, local copies, waits for them, and re-layouts: 9.44 us -> none  [gather_in_order(): parts.transpose(*turned, *range(len(sequence), parts.ndim))]
    all_to_all x0 -> x2, starting transfers between devices: none -> 9.17 us  [gather_in_order(): lax.all_to_all(jnp.stack([parts] * lax.axis_size(axes[k])), axes[k], 0, 0)]
  transfers between devices with their start and end apart: 17 -> 13, of which waited for: 17 -> 13; matrix products, arithmetic and copies ran while one was open for 2% -> 2% of each run, Pallas kernels for 0% -> 0%
where the time goes in v1:
time: 533 us; the launch traced here: 528 us
  blocking collectives  305 us (57%)
  waiting for transfers between devices  129 us (24%)
  local copies, waits for them, and re-layouts  37.7 us (7%)
  matrix products  23.5 us (4%)
  starting transfers between devices  16.9 us (3%)
  other arithmetic  15.3 us (3%)
    all_to_all x10, blocking collectives, gather_in_order(): lax.all_to_all(jnp.stack([parts] * lax.axis_size(axes[k])), axes[k], 0, 0)  305 us
    all_to_all x2, waiting for transfers between devices, gather_in_order(): lax.all_to_all(jnp.stack([parts] * lax.axis_size(axes[k])), axes[k], 0, 0)  89.8 us
    ppermute x9, waiting for transfers between devices, partner_2(): lax.ppermute(x, axis, [(i, i ^ 1 << distance) for i in range(lax.axis_siz...  37.9 us
    convert_element_type x3, local copies, waits for them, and re-layouts, apply_layer(): (whole_floats * scale * gain_row.astype(jnp.float32)).astype(jnp.bfloat16)  12.3 us
    transpose x3, local copies, waits for them, and re-layouts, joined_along(): return jnp.moveaxis(parts, 0, dim).reshape(lengths)  12.3 us
  transfers between devices with their start and end apart: 13, of which 13 were waited for; matrix products, arithmetic and copies ran while one was open for 2% of the time, Pallas kernels for 0%

profile of v1, /device:TPU:514, one launch (start us, length us, event | category | flops | bytes accessed | tf_op | source)
XLA Modules:
  0.0 528.2 jit_solution(13742891630461313655)
XLA Ops:
  1.0 30.9 %all_to_all.60 = bf16[8,1,128,128]{3,2,1,0:T(8,128)(2,1)S(1)} all-to-all(bf16[8,1,128,128]{3,2,1,0:T(8,128)(2,1)S(1)} %stack.72), channel_id=1, replica_groups=mesh['groups'=2,'section'=2,'mesh_0'=8,'mesh_1'=8] {'mesh_0'}, dimensions={0} | all-to-all | bytes 524288 | tf_op jit(solution)/shard_map/all_to_all | solution.py:24
  33.7 4.7 all-to-all-start.1
  39.8 43.1 %all-to-all-done.1 = bf16[8,8,128,128]{3,2,1,0:T(8,128)(2,1)} async-done(((bf16[8,8,128,128]{3,2,1,0:T(8,128)(2,1)}), bf16[8,8,128,128]{3,2,1,0:T(8,128)(2,1)}, u32[]{:S(2)}, u32[]{:S(2)}) %all-to-all-start.1) | async-done | bytes 2097184 | tf_op jit(solution)/shard_map/all_to_all | solution.py:24
  85.0 3.8 fusion.8
  88.9 4.2 copy.18
  95.7 3.1 collective-permute-done
  99.3 2.4 fusion.19
  104.4 7.3 %collective-permute-done.2 = bf16[128,128]{0,1:T(8,128)(2,1)S(1)} collective-permute-done((bf16[128,128]{0,1:T(8,128)(2,1)S(1)}, bf16[128,128]{0,1:T(8,128)(2,1)S(1)}, u32[]{:S(2)}, u32[]{:S(2)}) %collective-permute-start.2) | collective-permute-done | bytes 32800 | tf_op jit(solution)/shard_map/ppermute | solution.py:37
  112.3 14.5 %all_to_all.61 = bf16[8,1,128,128]{3,2,1,0:T(8,128)(2,1)S(1)} all-to-all(bf16[8,1,128,128]{3,2,1,0:T(8,128)(2,1)S(1)} %stack.80), channel_id=1, replica_groups=mesh['groups'=2,'section'=2,'mesh_0'=8,'mesh_1'=8] {'mesh_0'}, dimensions={0} | all-to-all | bytes 524288 | tf_op jit(solution)/shard_map/all_to_all | solution.py:24
  127.2 46.4 %all_to_all.62 = bf16[8,8,128,128]{3,2,1,0:T(8,128)(2,1)S(1)} all-to-all(bf16[8,8,128,128]{3,2,1,0:T(8,128)(2,1)S(1)} %stack.81), channel_id=1, replica_groups=mesh['groups'=2,'section'=2,'mesh_0'=8,'mesh_1'=8] {'mesh_1'}, dimensions={0} | all-to-all | bytes 4194304 | tf_op jit(solution)/shard_map/all_to_all | solution.py:24
  175.2 4.1 copy.22
  179.3 3.0 fusion.27
  184.5 15.5 %all_to_all.63 = bf16[8,1,128,128]{3,2,1,0:T(8,128)(2,1)S(1)} all-to-all(bf16[8,1,128,128]{3,2,1,0:T(8,128)(2,1)S(1)} %stack.83), channel_id=1, replica_groups=mesh['groups'=2,'section'=2,'mesh_0'=8,'mesh_1'=8] {'mesh_0'}, dimensions={0} | all-to-all | bytes 524288 | tf_op jit(solution)/shard_map/all_to_all | solution.py:24
  200.5 52.1 %all_to_all.64 = bf16[8,8,128,128]{3,2,1,0:T(8,128)(2,1)S(1)} all-to-all(bf16[8,8,128,128]{3,2,1,0:T(8,128)(2,1)S(1)} %stack.84), channel_id=1, replica_groups=mesh['groups'=2,'section'=2,'mesh_0'=8,'mesh_1'=8] {'mesh_1'}, dimensions={0} | all-to-all | bytes 4194304 | tf_op jit(solution)/shard_map/all_to_all | solution.py:24
  256.1 4.1 copy.24
  263.2 3.1 collective-permute-done.4
  271.7 7.4 %collective-permute-done.6 = bf16[128,128]{0,1:T(8,128)(2,1)S(1)} collective-permute-done((bf16[128,128]{0,1:T(8,128)(2,1)S(1)}, bf16[128,128]{0,1:T(8,128)(2,1)S(1)}, u32[]{:S(2)}, u32[]{:S(2)}) %collective-permute-start.6) | collective-permute-done | bytes 32800 | tf_op jit(solution)/shard_map/ppermute | solution.py:37
  279.7 14.5 %all_to_all.65 = bf16[8,1,128,128]{3,2,1,0:T(8,128)(2,1)S(1)} all-to-all(bf16[8,1,128,128]{3,2,1,0:T(8,128)(2,1)S(1)} %stack.85), channel_id=1, replica_groups=mesh['groups'=2,'section'=2,'mesh_0'=8,'mesh_1'=8] {'mesh_0'}, dimensions={0} | all-to-all | bytes 524288 | tf_op jit(solution)/shard_map/all_to_all | solution.py:24
  294.7 49.2 %all_to_all.66 = bf16[8,8,128,128]{3,2,1,0:T(8,128)(2,1)S(1)} all-to-all(bf16[8,8,128,128]{3,2,1,0:T(8,128)(2,1)S(1)} %stack.86), channel_id=1, replica_groups=mesh['groups'=2,'section'=2,'mesh_0'=8,'mesh_1'=8] {'mesh_1'}, dimensions={0} | all-to-all | bytes 4194304 | tf_op jit(solution)/shard_map/all_to_all | solution.py:24
  345.5 4.1 copy.26
  349.5 3.0 add_convert_fusion.1
  354.7 15.5 %all_to_all.67 = bf16[8,1,128,128]{3,2,1,0:T(8,128)(2,1)S(1)} all-to-all(bf16[8,1,128,128]{3,2,1,0:T(8,128)(2,1)S(1)} %stack.88), channel_id=1, replica_groups=mesh['groups'=2,'section'=2,'mesh_0'=8,'mesh_1'=8] {'mesh_0'}, dimensions={0} | all-to-all | bytes 524288 | tf_op jit(solution)/shard_map/all_to_all | solution.py:24
  370.7 52.1 %all_to_all.68 = bf16[8,8,128,128]{3,2,1,0:T(8,128)(2,1)S(1)} all-to-all(bf16[8,8,128,128]{3,2,1,0:T(8,128)(2,1)S(1)} %stack.89), channel_id=1, replica_groups=mesh['groups'=2,'section'=2,'mesh_0'=8,'mesh_1'=8] {'mesh_1'}, dimensions={0} | all-to-all | bytes 4194304 | tf_op jit(solution)/shard_map/all_to_all | solution.py:24
  426.4 4.1 copy.28
  433.2 3.1 collective-permute-done.8
  441.7 7.4 %collective-permute-done.10 = bf16[128,128]{0,1:T(8,128)(2,1)S(1)} collective-permute-done((bf16[128,128]{0,1:T(8,128)(2,1)S(1)}, bf16[128,128]{0,1:T(8,128)(2,1)S(1)}, u32[]{:S(2)}, u32[]{:S(2)}) %collective-permute-start.10) | collective-permute-done | bytes 32800 | tf_op jit(solution)/shard_map/ppermute | solution.py:37
  449.8 14.5 %all_to_all.69 = bf16[8,1,128,128]{3,2,1,0:T(8,128)(2,1)S(1)} all-to-all(bf16[8,1,128,128]{3,2,1,0:T(8,128)(2,1)S(1)} %stack.90), channel_id=1, replica_groups=mesh['groups'=2,'section'=2,'mesh_0'=8,'mesh_1'=8] {'mesh_0'}, dimensions={0} | all-to-all | bytes 524288 | tf_op jit(solution)/shard_map/all_to_all | solution.py:24
  466.1 4.5 all-to-all-start.11
  470.6 46.7 %all-to-all-done.11 = bf16[8,8,128,128]{3,2,1,0:T(8,128)(2,1)} async-done(((bf16[8,8,128,128]{3,2,1,0:T(8,128)(2,1)}), bf16[8,8,128,128]{3,2,1,0:T(8,128)(2,1)}, u32[]{:S(2)}, u32[]{:S(2)}) %all-to-all-start.11) | async-done | bytes 2097184 | tf_op jit(solution)/shard_map/all_to_all | solution.py:24
  517.3 3.1 copy.29
  520.4 4.1 copy.30
  524.5 3.0 fusion.71
  (107 shorter events, 49.4 us)
Async XLA Ops:
  0.0 99.3 %copy-start = (bf16[1,1,8192,128]{3,2,1,0:T(8,128)(2,1)S(1)}, bf16[1,1,8192,128]{3,2,1,0:T(8,128)(2,1)}, u32[]{:S(2)}) copy-start(bf16[1,1,8192,128]{3,2,1,0:T(8,128)(2,1)} %param.9) | copy-start | bytes 6291460
  33.6 4.7 copy-start.3
  33.7 4.7 copy-start.4
  33.7 49.3 %all-to-all-start.1 = ((bf16[8,8,128,128]{3,2,1,0:T(8,128)(2,1)}), bf16[8,8,128,128]{3,2,1,0:T(8,128)(2,1)}, u32[]{:S(2)}, u32[]{:S(2)}) async-start(bf16[8,8,128,128]{3,2,1,0:T(8,128)(2,1)} %stack.73), calls=%async_computation.1 | async-start | bytes 4194304 | tf_op jit(solution)/shard_map/all_to_all | solution.py:24
  88.9 4.2 copy-start.1
  95.1 3.8 collective-permute-start
  98.9 4.9 collective-permute-start.1
  103.8 7.9 %collective-permute-start.2 = (bf16[128,128]{0,1:T(8,128)(2,1)S(1)}, bf16[128,128]{0,1:T(8,128)(2,1)S(1)}, u32[]{:S(2)}, u32[]{:S(2)}) collective-permute-start(bf16[128,128]{0,1:T(8,128)(2,1)S(1)} %maximum_select_fusion.3), channel_id=1, source_target_pairs={{0,4},{1,5},{2,6},{3,7},{4,0},{5,1},{6,2},{7,3},{8,12},{9,13},{10,... | collective-permute-start | bytes 98312 | tf_op jit(solution)/shard_map/ppermute | solution.py:37
  179.2 5.2 copy-start.2
  182.3 2.2 collective-permute-start.3
  262.3 4.0 collective-permute-start.4
  266.2 4.9 collective-permute-start.5
  271.2 8.0 %collective-permute-start.6 = (bf16[128,128]{0,1:T(8,128)(2,1)S(1)}, bf16[128,128]{0,1:T(8,128)(2,1)S(1)}, u32[]{:S(2)}, u32[]{:S(2)}) collective-permute-start(bf16[128,128]{0,1:T(8,128)(2,1)S(1)} %maximum_select_fusion.4), channel_id=1, source_target_pairs={{0,4},{1,5},{2,6},{3,7},{4,0},{5,1},{6,2},{7,3},{8,12},{9,13},{10,... | collective-permute-start | bytes 98312 | tf_op jit(solution)/shard_map/ppermute | solution.py:37
  352.5 2.2 collective-permute-start.7
  432.5 3.8 collective-permute-start.8
  436.3 4.9 collective-permute-start.9
  441.2 8.0 %collective-permute-start.10 = (bf16[128,128]{0,1:T(8,128)(2,1)S(1)}, bf16[128,128]{0,1:T(8,128)(2,1)S(1)}, u32[]{:S(2)}, u32[]{:S(2)}) collective-permute-start(bf16[128,128]{0,1:T(8,128)(2,1)S(1)} %maximum_select_fusion.5), channel_id=1, source_target_pairs={{0,4},{1,5},{2,6},{3,7},{4,0},{5,1},{6,2},{7,3},{8,12},{9,13},{10,... | collective-permute-start | bytes 98312 | tf_op jit(solution)/shard_map/ppermute | solution.py:37
  466.1 51.2 %all-to-all-start.11 = ((bf16[8,8,128,128]{3,2,1,0:T(8,128)(2,1)}), bf16[8,8,128,128]{3,2,1,0:T(8,128)(2,1)}, u32[]{:S(2)}, u32[]{:S(2)}) async-start(bf16[8,8,128,128]{3,2,1,0:T(8,128)(2,1)} %stack.91), calls=%async_computation.11 | async-start | bytes 4194304 | tf_op jit(solution)/shard_map/all_to_all | solution.py:24
